TPU v7x, 32 devices: a whole 2x2x4 slice. The times are simulated.
32 devices in a mesh: blk: 8 (over z, x), shard: 4 (over y, core).
Axes of the slice: x: 2, y: 2, z: 4, core: 2. Of those that a mesh axis runs over, the one named last changes fastest.
Arguments:
- tokens: bfloat16 [8192, 2048], P(('blk', 'shard')), may hold values from -6 to 6
- targets: bfloat16 [8192, 2048], P(('blk', 'shard')), may hold values from -6 to 6
- up_weight: bfloat16 [2048, 7168], P(None, 'shard'), may hold values from -0.125 to 0.125
- down_weight: bfloat16 [8, 7168, 2048], P('blk', 'shard'), may hold values from -6 to 6
- mix_numer: int32 [2, 8, 3], replicated, may hold values from 1 to 2, as said below
Outputs:
- drift: bfloat16 [8, 7168, 2048], P('blk', 'shard')
Inputs may be any that keep to these rules, and one draw needn't show every extreme that they name: Each row of mix_numer is (2, 1, 1), (1, 2, 1) or (1, 1, 2).
All inputs are finite; a program needn't handle non-finite values.
Results may differ from a plain program's by a relative error of at most 0.017.
Values may be sent and summed in bfloat16 or wider, within the bound.
A program may use at most 128 MiB of HBM per device.

v0:
```python
import functools
import math

import jax
import jax.numpy as jnp
from jax import lax
from jax.experimental import pallas as pl
from jax.experimental.pallas import tpu as pltpu
from jax.sharding import PartitionSpec as P

learn_rate = 2.0
MESH = pl.DeviceIdType.MESH
UPTILE = 256
LAG_MIX = 3
ROWTILE = 16


def silu(v):
    return v / (1.0 + jnp.exp(-v))


def kernel(
    workers, shards, rs, cs,
    tokens, targets, up_hbm, w_hbm, numer, out,
    tok, up, w, tgt, hid, hidt, own, part, rsl, res, land,
    load_sem, tok_send, tok_recv, rs_send, rs_recv, ag_send, ag_recv,
    a2a_send, a2a_recv, ret_send, ret_recv,
):
    blk = lax.axis_index("blk")
    me = lax.axis_index("shard")
    sib = me + 1 - 2 * (me % 2)
    trows = tokens.shape[0]
    width = tokens.shape[1]
    ff = hidt.shape[0]
    chunks, chunk = w.shape[0], w.shape[2]
    pr, pc = ff // rs, chunk // cs
    far = shards // 2 - 1
    scale = jnp.float32(1.0 / math.sqrt(ff * shards))

    own_tok = pltpu.make_async_copy(tokens, tok.at[me], load_sem.at[0])
    own_tok.start()
    up_copy = pltpu.make_async_copy(up_hbm, up, load_sem.at[1])
    up_copy.start()

    barrier = pltpu.get_barrier_semaphore()

    def greet_blk(i, c):
        pl.semaphore_signal(
            barrier, inc=1, device_id={"blk": (blk + i) % workers}, device_id_type=MESH)
        return c

    lax.fori_loop(1, workers, greet_blk, 0)
    for i in range(1, shards):
        pl.semaphore_signal(
            barrier, inc=1, device_id={"shard": (me + i) % shards}, device_id_type=MESH)
    pl.semaphore_wait(barrier, workers - 1 + shards - 1)

    def tok_copy(src, which, owner, to):
        return pltpu.make_async_remote_copy(
            src_ref=src, dst_ref=tok.at[owner],
            send_sem=tok_send.at[which], recv_sem=tok_recv.at[which],
            device_id={"shard": to}, device_id_type=MESH)

    first = [tok_copy(tokens, d, me, (me + 2 * d) % shards) for d in range(1, far + 1)]
    for c in first:
        c.start()
    to_sib = tok_copy(tokens, 0, me, sib)
    to_sib.start()

    def w_copy(j):
        return pltpu.make_async_copy(
            w_hbm.at[:, pl.ds(pl.multiple_of(j * chunk, chunk), chunk)], w.at[j], load_sem.at[3 + j])

    tgt_copy = pltpu.make_async_copy(targets, tgt, load_sem.at[2])
    tgt_copy.start()
    for j in range(chunks):
        w_copy(j).start()

    def hidden_of(q):
        def tile(n, c):
            cols = pl.ds(pl.multiple_of(n * UPTILE, UPTILE), UPTILE)
            v = silu(jnp.dot(tok[q], up[:, cols], preferred_element_type=jnp.float32))
            hid[q, :, cols] = v.astype(jnp.bfloat16)
            hidt[cols, pl.ds(pl.multiple_of(q * trows, trows), trows)] = v.T.astype(jnp.bfloat16)
            return c

        lax.fori_loop(0, ff // UPTILE, tile, 0)

    own_tok.wait()
    up_copy.wait()
    hidden_of(me)
    to_sib.wait_recv()
    hidden_of(sib)
    forwards = []
    for d in range(1, far + 1):
        src = (me - 2 * d + 2 * shards) % shards
        first[d - 1].wait_recv()
        f = tok_copy(tok.at[src], far + d, src, sib)
        f.start()
        forwards.append(f)
        hidden_of(src)
    for d in range(1, far + 1):
        forwards[d - 1].wait_recv()
        hidden_of((sib - 2 * d + 2 * shards) % shards)

    tgt_copy.wait()

    def rs_copy(j, i):
        return pltpu.make_async_remote_copy(
            src_ref=part.at[j, i - 1], dst_ref=rsl.at[j, i - 1],
            send_sem=rs_send.at[j, i - 1], recv_sem=rs_recv.at[j, i - 1],
            device_id={"shard": (me + i) % shards}, device_id_type=MESH)

    def stage_out(j):
        w_copy(j).wait()

        def one(n, c):
            i = n + 1
            q = (me + i) % shards
            v = jnp.dot(hid[q], w[j], preferred_element_type=jnp.float32) * scale

            @pl.when(i < shards)
            def _():
                part[j, i - 1] = v.astype(jnp.bfloat16)
                rs_copy(j, i).start()

            @pl.when(i == shards)
            def _():
                own[j % 4] = v

            return c

        lax.fori_loop(0, shards, one, 0)

    def ag_copy(j, i):
        return pltpu.make_async_remote_copy(
            src_ref=res.at[j, me], dst_ref=res.at[j, me],
            send_sem=ag_send.at[j, i - 1], recv_sem=ag_recv.at[j, i - 1],
            device_id={"shard": (me + i) % shards}, device_id_type=MESH)

    def stage_resid(j):
        for i in range(1, shards):
            rs_copy(j, i).wait_recv()
        total = own[j % 4]
        for i in range(1, shards):
            total = total + rsl[j, i - 1].astype(jnp.float32)
        cols = pl.ds(pl.multiple_of(j * chunk, chunk), chunk)
        res[j, me] = (total - tgt[:, cols].astype(jnp.float32)).astype(jnp.bfloat16)
        for i in range(1, shards):
            ag_copy(j, i).start()

    def place(k):
        r = pl.ds(pl.multiple_of((k // cs) * pr, 16), pr)
        return r, (k % cs) * pc

    half = workers // 2
    mine = blk // half

    def peer(i):
        here = (i - 1) // half
        side = (mine + 1 + here) % 2
        return side * half + (blk + (i - 1) - here * (half - 1)) % half

    def a2a_copy(j, k, i):
        r, c0 = place(k)
        cols = pl.ds(0, pc) if cs == 1 else pl.ds(pl.multiple_of(c0, 128), pc)
        return pltpu.make_async_remote_copy(
            src_ref=w.at[j, r, cols], dst_ref=land.at[j, blk],
            send_sem=a2a_send.at[j, i], recv_sem=a2a_recv.at[j, i],
            device_id={"blk": k}, device_id_type=MESH)

    def stage_step(j):
        for i in range(1, shards):
            ag_copy(j, i).wait_recv()

        def one(n, c):
            i = n + 1
            k = peer(i)
            r, c0 = place(k)
            cols = pl.ds(0, pc) if cs == 1 else pl.ds(pl.multiple_of(c0, 128), pc)
            rhs = res[j].reshape(shards * trows, chunk) if cs == 1 else (
                res[j, :, :, cols].reshape(shards * trows, pc))
            grad = jnp.dot(hidt[r, :], rhs, preferred_element_type=jnp.float32)
            new = (w[j, r, cols].astype(jnp.float32) - (learn_rate * scale) * grad).astype(jnp.bfloat16)

            @pl.when(i < workers)
            def _():
                w[j, r, cols] = new
                a2a_copy(j, k, i).start()

            @pl.when(i == workers)
            def _():
                land[j, blk] = new

            return c

        lax.fori_loop(0, workers, one, 0)

    def out_at(j, k):
        r, c0 = place(k)
        return out.at[r, pl.ds(pl.multiple_of(j * chunk + c0, 128), pc)]

    def ret_copy(j, i):
        k = peer(i)
        return pltpu.make_async_remote_copy(
            src_ref=land.at[j, k], dst_ref=out_at(j, blk),
            send_sem=ret_send.at[j, i], recv_sem=ret_recv.at[j, i],
            device_id={"blk": k}, device_id_type=MESH)

    def own_copy(j):
        return pltpu.make_async_copy(land.at[j, blk], out_at(j, blk), ret_send.at[j, 0])

    rounds = numer.shape[0]

    def stage_mix(j):
        def arrived(i, c):
            a2a_copy(j, peer(i), i).wait_recv()
            return c

        lax.fori_loop(1, workers, arrived, 0)
        coef = [
            [[numer[r, k, e].astype(jnp.float32) * 0.25 for e in range(3)] for k in range(workers)]
            for r in range(rounds)
        ]

        def tile(t, c):
            rows = pl.ds(pl.multiple_of(t * ROWTILE, ROWTILE), ROWTILE)
            cur = [land[j, k, rows, :].astype(jnp.float32) for k in range(workers)]
            for r in range(rounds):
                cur = [
                    (
                        coef[r][k][0] * cur[k]
                        + coef[r][k][1] * cur[(k - 1) % workers]
                        + coef[r][k][2] * cur[(k + 1) % workers]
                    ).astype(jnp.bfloat16).astype(jnp.float32)
                    for k in range(workers)
                ]
            total = functools.reduce(lambda a, b: a + b, cur)
            average = total * jnp.float32(1.0 / workers)
            for k in range(workers):
                land[j, k, rows, :] = (cur[k] - average).astype(jnp.bfloat16)
            return c

        lax.fori_loop(0, pr // ROWTILE, tile, 0)

        def give(i, c):
            ret_copy(j, i).start()
            return c

        lax.fori_loop(1, workers, give, 0)
        own_copy(j).start()

    def step(t, c):
        @pl.when(t < chunks)
        def _():
            stage_out(t)

        @pl.when((t >= 1) & (t - 1 < chunks))
        def _():
            stage_step(t - 1)

        @pl.when(t < chunks)
        def _():
            stage_resid(t)

        @pl.when(t >= LAG_MIX)
        def _():
            stage_mix(t - LAG_MIX)

        return c

    lax.fori_loop(0, chunks + LAG_MIX, step, 0)

    to_sib.wait_send()
    for c in first + forwards:
        c.wait_send()

    def finish(j, c):
        for i in range(1, shards):
            rs_copy(j, i).wait_send()
            ag_copy(j, i).wait_send()

        def one(i, c):
            a2a_copy(j, peer(i), i).wait_send()
            r = ret_copy(j, i)
            r.wait_send()
            r.wait_recv()
            return c

        lax.fori_loop(1, workers, one, 0)
        own_copy(j).wait()
        return c

    lax.fori_loop(0, chunks, finish, 0)


def solution(mesh):
    workers, shards = mesh.shape["blk"], mesh.shape["shard"]

    def body(tokens, targets, up_weight, down_weight, mix_numer):
        weight = down_weight[0]
        ff, d = weight.shape
        trows = tokens.shape[0]

        rs = math.gcd(workers, ff // 16)
        cs = workers // rs
        chunk = 128 * cs
        chunks = d // chunk
        pr, pc = ff // rs, chunk // cs
        far = shards // 2 - 1
        bf = jnp.bfloat16
        dma = pltpu.SemaphoreType.DMA
        any_ref = pl.BlockSpec(memory_space=pltpu.HBM)
        out = pl.pallas_call(
            functools.partial(kernel, workers, shards, rs, cs),
            out_shape=jax.ShapeDtypeStruct((ff, d), bf),
            in_specs=[any_ref] * 4 + [pl.BlockSpec(memory_space=pltpu.SMEM)],
            out_specs=any_ref,
            scratch_shapes=[
                pltpu.VMEM((shards, trows, d), bf),
                pltpu.VMEM((d, ff), bf),
                pltpu.VMEM((chunks, ff, chunk), bf),
                pltpu.VMEM((trows, d), bf),
                pltpu.VMEM((shards, trows, ff), bf),
                pltpu.VMEM((ff, shards * trows), bf),
                pltpu.VMEM((4, trows, chunk), jnp.float32),
                pltpu.VMEM((chunks, shards - 1, trows, chunk), bf),
                pltpu.VMEM((chunks, shards - 1, trows, chunk), bf),
                pltpu.VMEM((chunks, shards, trows, chunk), bf),
                pltpu.VMEM((chunks, workers, pr, pc), bf),
                dma((3 + chunks,)),
                dma((2 * far + 1,)),
                dma((2 * far + 1,)),
                dma((chunks, shards - 1)),
                dma((chunks, shards - 1)),
                dma((chunks, shards - 1)),
                dma((chunks, shards - 1)),
                dma((chunks, workers)),
                dma((chunks, workers)),
                dma((chunks, workers)),
                dma((chunks, workers)),
            ],
            compiler_params=pltpu.CompilerParams(
                collective_id=0, has_side_effects=True, vmem_limit_bytes=66 * 1024 * 1000
            ),
        )(tokens, targets, up_weight, weight, mix_numer)
        return out[None]

    in_specs = (
        P(("blk", "shard"), None),
        P(("blk", "shard"), None),
        P(None, "shard"),
        P("blk", "shard", None),
        P(),
    )
    return jax.shard_map(
        body, mesh=mesh, in_specs=in_specs, out_specs=P("blk", "shard", None), check_vma=False
    )
```

profile of v0, /device:TPU:0, one launch (start us, length us, event | category | flops | bytes accessed | tf_op | source)
XLA Modules:
  0.0 379.2 jit_solution(17554087980561915665)
XLA Ops:
  0.0 1.4 copy.6.numer
  1.4 370.3 %shard_map.55 = bf16[1792,2048]{1,0:T(8,128)(2,1)} custom-call(bf16[256,2048]{1,0:T(8,128)(2,1)} %tokens.1, bf16[256,2048]{1,0:T(8,128)(2,1)} %targets.1, bf16[2048,1792]{1,0:T(8,128)(2,1)} %up_hbm.1, bf16[1792,2048]{1,0:T(8,128)(2,1)} %bitcast.3, s32[2,8,3]{2,1,0:T(8,128)} %copy.6.numer), custom_call_target="tpu_custom_call" | custom-call | tf_op jit(solution)/shard_map/pallas_call | solution.py:314
  371.6 7.5 %copy.8 = bf16[1,1792,2048]{2,1,0:T(8,128)(2,1)} copy(bf16[1,1792,2048]{2,1,0:T(8,128)(2,1)} %bitcast.2) | data formatting | bytes 14680064
where the time goes:
time: 379 us
  Pallas kernels  370 us (98%)
  local copies, waits for them, and re-layouts  8.89 us (2%)
    pallas_call x1, Pallas kernels, body(): pl.pallas_call(functools.partial(kernel, workers, shards, rs, cs), out_sh...  370 us
    unnamed x2, local copies, waits for them, and re-layouts  8.89 us

commit v1 on v0

--- a/solution.py
+++ b/solution.py
@@ -210,7 +210,7 @@
     def own_copy(j):
         return pltpu.make_async_copy(land.at[j, blk], out_at(j, blk), ret_send.at[j, 0])
 
-    rounds = numer.shape[0]
+    rounds = numer.shape[1]
 
     def stage_mix(j):
         def arrived(i, c):
@@ -219,7 +219,7 @@
 
         lax.fori_loop(1, workers, arrived, 0)
         coef = [
-            [[numer[r, k, e].astype(jnp.float32) * 0.25 for e in range(3)] for k in range(workers)]
+            [[numer[e, r, k].astype(jnp.float32) * 0.25 for e in range(3)] for k in range(workers)]
             for r in range(rounds)
         ]
 
@@ -313,9 +313,9 @@
         any_ref = pl.BlockSpec(memory_space=pltpu.HBM)
         out = pl.pallas_call(
             functools.partial(kernel, workers, shards, rs, cs),
-            out_shape=jax.ShapeDtypeStruct((ff, d), bf),
+            out_shape=pltpu.VMEM((ff, d), bf),
             in_specs=[any_ref] * 4 + [pl.BlockSpec(memory_space=pltpu.SMEM)],
-            out_specs=any_ref,
+            out_specs=pl.BlockSpec(memory_space=pltpu.VMEM),
             scratch_shapes=[
                 pltpu.VMEM((shards, trows, d), bf),
                 pltpu.VMEM((d, ff), bf),
@@ -341,9 +341,9 @@
                 dma((chunks, workers)),
             ],
             compiler_params=pltpu.CompilerParams(
-                collective_id=0, has_side_effects=True, vmem_limit_bytes=66 * 1024 * 1000
+                collective_id=0, has_side_effects=True, vmem_limit_bytes=54 * 1024 * 1000
             ),
-        )(tokens, targets, up_weight, weight, mix_numer)
+        )(tokens, targets, up_weight, weight, jnp.transpose(mix_numer, (2, 0, 1)))
         return out[None]
 
     in_specs = (

time: 379 us -> 373 us (0.984)
  local copies, waits for them, and re-layouts: 8.89 us -> 3.05 us
    unnamed x2 -> x1, local copies, waits for them, and re-layouts: 8.89 us -> 3.05 us
where the time goes in v1:
time: 373 us
  Pallas kernels  370 us (99%)
    pallas_call x1, Pallas kernels, body(): pl.pallas_call(functools.partial(kernel, workers, shards, rs, cs), out_sh...  370 us

profile of v1, /device:TPU:0, one launch (start us, length us, event | category | flops | bytes accessed | tf_op | source)
XLA Modules:
  0.0 373.2 jit_solution(1904594038156810567)
XLA Ops:
  0.0 370.1 %shard_map.55 = bf16[1792,2048]{1,0:T(8,128)(2,1)S(1)} custom-call(bf16[256,2048]{1,0:T(8,128)(2,1)} %tokens.1, bf16[256,2048]{1,0:T(8,128)(2,1)} %targets.1, bf16[2048,1792]{1,0:T(8,128)(2,1)} %up_hbm.1, bf16[1792,2048]{1,0:T(8,128)(2,1)} %bitcast.4, s32[3,2,8]{2,1,0:T(2,128)} %bitcast.5), custom_call_target="tpu_custom_call" | custom-call | tf_op jit(solution)/shard_map/pallas_call | solution.py:314
  370.1 3.1 copy.7

commit v2 on v1

--- a/solution.py
+++ b/solution.py
@@ -24,7 +24,7 @@
     tokens, targets, up_hbm, w_hbm, numer, out,
     tok, up, w, tgt, hid, hidt, own, part, rsl, res, land,
     load_sem, tok_send, tok_recv, rs_send, rs_recv, ag_send, ag_recv,
-    a2a_send, a2a_recv, ret_send, ret_recv,
+    a2a_send, a2a_recv, ret_send, ret_recv, own_sem,
 ):
     blk = lax.axis_index("blk")
     me = lax.axis_index("shard")
@@ -43,6 +43,9 @@
     up_copy.start()
 
     barrier = pltpu.get_barrier_semaphore()
+
+    def await_bytes(ref, sem):
+        pltpu.make_async_copy(ref, ref, sem).wait()
 
     def greet_blk(i, c):
         pl.semaphore_signal(
@@ -108,7 +111,7 @@
     def rs_copy(j, i):
         return pltpu.make_async_remote_copy(
             src_ref=part.at[j, i - 1], dst_ref=rsl.at[j, i - 1],
-            send_sem=rs_send.at[j, i - 1], recv_sem=rs_recv.at[j, i - 1],
+            send_sem=rs_send.at[0], recv_sem=rs_recv.at[j],
             device_id={"shard": (me + i) % shards}, device_id_type=MESH)
 
     def stage_out(j):
@@ -135,12 +138,11 @@
     def ag_copy(j, i):
         return pltpu.make_async_remote_copy(
             src_ref=res.at[j, me], dst_ref=res.at[j, me],
-            send_sem=ag_send.at[j, i - 1], recv_sem=ag_recv.at[j, i - 1],
+            send_sem=ag_send.at[0], recv_sem=ag_recv.at[j],
             device_id={"shard": (me + i) % shards}, device_id_type=MESH)
 
     def stage_resid(j):
-        for i in range(1, shards):
-            rs_copy(j, i).wait_recv()
+        await_bytes(rsl.at[j], rs_recv.at[j])
         total = own[j % 4]
         for i in range(1, shards):
             total = total + rsl[j, i - 1].astype(jnp.float32)
@@ -166,12 +168,11 @@
         cols = pl.ds(0, pc) if cs == 1 else pl.ds(pl.multiple_of(c0, 128), pc)
         return pltpu.make_async_remote_copy(
             src_ref=w.at[j, r, cols], dst_ref=land.at[j, blk],
-            send_sem=a2a_send.at[j, i], recv_sem=a2a_recv.at[j, i],
+            send_sem=a2a_send.at[0], recv_sem=a2a_recv.at[j],
             device_id={"blk": k}, device_id_type=MESH)
 
     def stage_step(j):
-        for i in range(1, shards):
-            ag_copy(j, i).wait_recv()
+        await_bytes(res.at[j, pl.ds(0, shards - 1)], ag_recv.at[j])
 
         def one(n, c):
             i = n + 1
@@ -204,20 +205,16 @@
         k = peer(i)
         return pltpu.make_async_remote_copy(
             src_ref=land.at[j, k], dst_ref=out_at(j, blk),
-            send_sem=ret_send.at[j, i], recv_sem=ret_recv.at[j, i],
+            send_sem=ret_send.at[0], recv_sem=ret_recv.at[0],
             device_id={"blk": k}, device_id_type=MESH)
 
     def own_copy(j):
-        return pltpu.make_async_copy(land.at[j, blk], out_at(j, blk), ret_send.at[j, 0])
+        return pltpu.make_async_copy(land.at[j, blk], out_at(j, blk), own_sem.at[0])
 
     rounds = numer.shape[1]
 
     def stage_mix(j):
-        def arrived(i, c):
-            a2a_copy(j, peer(i), i).wait_recv()
-            return c
-
-        lax.fori_loop(1, workers, arrived, 0)
+        await_bytes(land.at[j, pl.ds(0, workers - 1)], a2a_recv.at[j])
         coef = [
             [[numer[e, r, k].astype(jnp.float32) * 0.25 for e in range(3)] for k in range(workers)]
             for r in range(rounds)
@@ -275,23 +272,13 @@
     for c in first + forwards:
         c.wait_send()
 
-    def finish(j, c):
-        for i in range(1, shards):
-            rs_copy(j, i).wait_send()
-            ag_copy(j, i).wait_send()
-
-        def one(i, c):
-            a2a_copy(j, peer(i), i).wait_send()
-            r = ret_copy(j, i)
-            r.wait_send()
-            r.wait_recv()
-            return c
-
-        lax.fori_loop(1, workers, one, 0)
-        own_copy(j).wait()
-        return c
-
-    lax.fori_loop(0, chunks, finish, 0)
+    await_bytes(part, rs_send.at[0])
+    await_bytes(res.at[:, pl.ds(0, shards - 1)], ag_send.at[0])
+    away = land.at[:, pl.ds(0, workers - 1)]
+    await_bytes(away, a2a_send.at[0])
+    await_bytes(away, ret_send.at[0])
+    await_bytes(away, ret_recv.at[0])
+    await_bytes(land.at[:, 0], own_sem.at[0])
 
 
 def solution(mesh):
@@ -331,14 +318,15 @@
                 dma((3 + chunks,)),
                 dma((2 * far + 1,)),
                 dma((2 * far + 1,)),
-                dma((chunks, shards - 1)),
-                dma((chunks, shards - 1)),
-                dma((chunks, shards - 1)),
-                dma((chunks, shards - 1)),
-                dma((chunks, workers)),
-                dma((chunks, workers)),
-                dma((chunks, workers)),
-                dma((chunks, workers)),
+                dma((1,)),
+                dma((chunks,)),
+                dma((1,)),
+                dma((chunks,)),
+                dma((1,)),
+                dma((chunks,)),
+                dma((1,)),
+                dma((1,)),
+                dma((1,)),
             ],
             compiler_params=pltpu.CompilerParams(
                 collective_id=0, has_side_effects=True, vmem_limit_bytes=54 * 1024 * 1000

time: 373 us -> 368 us (0.987)
  Pallas kernels: 370 us -> 364 us
    pallas_call x1, Pallas kernels: 370 us -> 364 us  [body(): pl.pallas_call(functools.partial(kernel, workers, shards, rs, cs), out_sh...]
where the time goes in v2:
time: 368 us; the launch traced here: 367 us
  Pallas kernels  364 us (99%)
    pallas_call x1, Pallas kernels, body(): pl.pallas_call(functools.partial(kernel, workers, shards, rs, cs), out_sh...  364 us

profile of v2, /device:TPU:0, one launch (start us, length us, event | category | flops | bytes accessed | tf_op | source)
XLA Modules:
  0.0 367.3 jit_solution(11136157750396283335)
XLA Ops:
  0.0 364.3 %shard_map.55 = bf16[1792,2048]{1,0:T(8,128)(2,1)S(1)} custom-call(bf16[256,2048]{1,0:T(8,128)(2,1)} %tokens.1, bf16[256,2048]{1,0:T(8,128)(2,1)} %targets.1, bf16[2048,1792]{1,0:T(8,128)(2,1)} %up_hbm.1, bf16[1792,2048]{1,0:T(8,128)(2,1)} %bitcast.4, s32[3,2,8]{2,1,0:T(2,128)} %bitcast.5), custom_call_target="tpu_custom_call" | custom-call | tf_op jit(solution)/shard_map/pallas_call | solution.py:301
  364.3 3.1 copy.7

commit v3 on v2

--- a/solution.py
+++ b/solution.py
@@ -11,7 +11,10 @@
 learn_rate = 2.0
 MESH = pl.DeviceIdType.MESH
 UPTILE = 256
-LAG_MIX = 3
+LAG_MIX = 4
+PIECES = 8
+HELPED = 3
+EARLY = 3
 ROWTILE = 16
 
 
@@ -22,8 +25,8 @@
 def kernel(
     workers, shards, rs, cs,
     tokens, targets, up_hbm, w_hbm, numer, out,
-    tok, up, w, tgt, hid, hidt, own, part, rsl, res, land,
-    load_sem, tok_send, tok_recv, rs_send, rs_recv, ag_send, ag_recv,
+    tok, up, w, tgt, hid, hidt, own, part, rsl, res, land, relay,
+    load_sem, tok_send, tok_recv, help_send, help_recv, rs_send, rs_recv, ag_send, ag_recv,
     a2a_send, a2a_recv, ret_send, ret_recv, own_sem,
 ):
     blk = lax.axis_index("blk")
@@ -56,19 +59,64 @@
     for i in range(1, shards):
         pl.semaphore_signal(
             barrier, inc=1, device_id={"shard": (me + i) % shards}, device_id_type=MESH)
-    pl.semaphore_wait(barrier, workers - 1 + shards - 1)
-
-    def tok_copy(src, which, owner, to):
-        return pltpu.make_async_remote_copy(
-            src_ref=src, dst_ref=tok.at[owner],
-            send_sem=tok_send.at[which], recv_sem=tok_recv.at[which],
+    quarter = workers // 4
+    helped = HELPED if workers % 4 == 0 and far == 1 else 0
+    inner = (blk >= quarter) & (blk < workers - quarter)
+    aside = jnp.where(blk < workers // 2, quarter, -quarter)
+    helper = {"blk": blk + jnp.where(inner, -aside, aside), "shard": (me + 2) % shards}
+    if helped:
+        pl.semaphore_signal(barrier, inc=1, device_id=helper, device_id_type=MESH)
+    pl.semaphore_wait(barrier, workers - 1 + shards - 1 + (1 if helped else 0))
+
+    prow = trows // PIECES
+
+    def rows_of(p):
+        return pl.ds(p * prow, prow)
+
+    def tok_copy(src, sem, owner, p, to):
+        return pltpu.make_async_remote_copy(
+            src_ref=src.at[rows_of(p)], dst_ref=tok.at[owner, rows_of(p)],
+            send_sem=tok_send.at[0], recv_sem=tok_recv.at[sem],
             device_id={"shard": to}, device_id_type=MESH)
 
-    first = [tok_copy(tokens, d, me, (me + 2 * d) % shards) for d in range(1, far + 1)]
-    for c in first:
-        c.start()
-    to_sib = tok_copy(tokens, 0, me, sib)
-    to_sib.start()
+    def direct(d, p):
+        return tok_copy(tokens, 1 + (2 * d - 2) * PIECES + p, me, p, (me + 2 * d) % shards)
+
+    def forward(d, p):
+        src = (me - 2 * d + 2 * shards) % shards
+        return tok_copy(tok.at[src], 1 + (2 * d - 1) * PIECES + p, src, p, sib)
+
+    def to_relay(p):
+        return pltpu.make_async_remote_copy(
+            src_ref=tokens.at[rows_of(p)], dst_ref=relay.at[p - PIECES + helped],
+            send_sem=tok_send.at[0], recv_sem=help_recv.at[p - PIECES + helped],
+            device_id=helper, device_id_type=MESH)
+
+    def from_relay(p):
+        owner = (me + 2) % shards
+        return pltpu.make_async_remote_copy(
+            src_ref=relay.at[p - PIECES + helped], dst_ref=tok.at[owner, rows_of(p)],
+            send_sem=help_send.at[0], recv_sem=tok_recv.at[1 + p],
+            device_id={"blk": blk + aside}, device_id_type=MESH)
+
+    sib_copy = pltpu.make_async_remote_copy(
+        src_ref=tokens, dst_ref=tok.at[me], send_sem=tok_send.at[0], recv_sem=tok_recv.at[0],
+        device_id={"shard": sib}, device_id_type=MESH)
+
+    def send_direct(last):
+        for p in range(last):
+            for d in range(1, far + 1):
+                direct(d, p).start()
+
+    if helped:
+        @pl.when(inner)
+        def _():
+            for p in range(PIECES - helped, PIECES):
+                to_relay(p).start()
+            send_direct(PIECES - helped)
+    else:
+        send_direct(PIECES)
+    sib_copy.start()
 
     def w_copy(j):
         return pltpu.make_async_copy(
@@ -79,34 +127,15 @@
     for j in range(chunks):
         w_copy(j).start()
 
-    def hidden_of(q):
-        def tile(n, c):
-            cols = pl.ds(pl.multiple_of(n * UPTILE, UPTILE), UPTILE)
-            v = silu(jnp.dot(tok[q], up[:, cols], preferred_element_type=jnp.float32))
-            hid[q, :, cols] = v.astype(jnp.bfloat16)
-            hidt[cols, pl.ds(pl.multiple_of(q * trows, trows), trows)] = v.T.astype(jnp.bfloat16)
+    def hidden_of(q, r0, n):
+        def tile(t, c):
+            cols = pl.ds(pl.multiple_of(t * UPTILE, UPTILE), UPTILE)
+            v = silu(jnp.dot(tok[q, r0:r0 + n], up[:, cols], preferred_element_type=jnp.float32))
+            hid[q, r0:r0 + n, cols] = v.astype(jnp.bfloat16)
+            hidt[cols, pl.ds(pl.multiple_of(q * trows + r0, 128), n)] = v.T.astype(jnp.bfloat16)
             return c
 
-        lax.fori_loop(0, ff // UPTILE, tile, 0)
-
-    own_tok.wait()
-    up_copy.wait()
-    hidden_of(me)
-    to_sib.wait_recv()
-    hidden_of(sib)
-    forwards = []
-    for d in range(1, far + 1):
-        src = (me - 2 * d + 2 * shards) % shards
-        first[d - 1].wait_recv()
-        f = tok_copy(tok.at[src], far + d, src, sib)
-        f.start()
-        forwards.append(f)
-        hidden_of(src)
-    for d in range(1, far + 1):
-        forwards[d - 1].wait_recv()
-        hidden_of((sib - 2 * d + 2 * shards) % shards)
-
-    tgt_copy.wait()
+        lax.fori_loop(0, ff // UPTILE, tile, 0, unroll=True)
 
     def rs_copy(j, i):
         return pltpu.make_async_remote_copy(
@@ -114,26 +143,77 @@
             send_sem=rs_send.at[0], recv_sem=rs_recv.at[j],
             device_id={"shard": (me + i) % shards}, device_id_type=MESH)
 
-    def stage_out(j):
+    near = (sib - me + shards) % shards
+
+    def out_of(q, j):
+        return jnp.dot(hid[q], w[j], preferred_element_type=jnp.float32) * scale
+
+    def give_out(j, i):
+        part[j, i - 1] = out_of((me + i) % shards, j).astype(jnp.bfloat16)
+        rs_copy(j, i).start()
+
+    def out_away(j):
+        def one(n, c):
+            give_out(j, 1 + n + jnp.where(n + 1 >= near, 1, 0))
+            return c
+
+        lax.fori_loop(0, shards - 2, one, 0)
+
+    def out_here(j):
+        give_out(j, near)
+        own[j % 4] = out_of(me, j)
+
+    def relay_one(p):
+        if helped:
+            @pl.when(jnp.logical_not(inner))
+            def _():
+                to_relay(p).wait_recv()
+                from_relay(p).start()
+
+    def pass_on(pieces):
+        for p in pieces:
+            for d in range(1, far + 1):
+                direct(d, p).wait_recv()
+                forward(d, p).start()
+
+    def passed_on(pieces):
+        for p in pieces:
+            for d in range(1, far + 1):
+                forward(d, p).wait_recv()
+
+    own_tok.wait()
+    up_copy.wait()
+    hidden_of(me, 0, trows)
+    for p in range(PIECES - helped, PIECES - 1):
+        relay_one(p)
+    sib_copy.wait_recv()
+    hidden_of(sib, 0, trows)
+    if helped:
+        relay_one(PIECES - 1)
+
+        @pl.when(jnp.logical_not(inner))
+        def _():
+            send_direct(PIECES)
+
+    h = PIECES // 2
+    for j in range(EARLY):
         w_copy(j).wait()
-
-        def one(n, c):
-            i = n + 1
-            q = (me + i) % shards
-            v = jnp.dot(hid[q], w[j], preferred_element_type=jnp.float32) * scale
-
-            @pl.when(i < shards)
-            def _():
-                part[j, i - 1] = v.astype(jnp.bfloat16)
-                rs_copy(j, i).start()
-
-            @pl.when(i == shards)
-            def _():
-                own[j % 4] = v
-
-            return c
-
-        lax.fori_loop(0, shards, one, 0)
+        out_here(j)
+        pass_on(range(h * j // EARLY, h * (j + 1) // EARLY))
+    mid = trows // 2
+    for d in range(1, far + 1):
+        hidden_of((me - 2 * d + 2 * shards) % shards, 0, mid)
+    passed_on(range(h))
+    for d in range(1, far + 1):
+        hidden_of((sib - 2 * d + 2 * shards) % shards, 0, mid)
+    pass_on(range(h, PIECES))
+    for d in range(1, far + 1):
+        hidden_of((me - 2 * d + 2 * shards) % shards, mid, trows - mid)
+    passed_on(range(h, PIECES))
+    for d in range(1, far + 1):
+        hidden_of((sib - 2 * d + 2 * shards) % shards, mid, trows - mid)
+
+    tgt_copy.wait()
 
     def ag_copy(j, i):
         return pltpu.make_async_remote_copy(
@@ -248,9 +328,17 @@
         own_copy(j).start()
 
     def step(t, c):
+        @pl.when((t < chunks) & (t >= EARLY))
+        def _():
+            w_copy(t).wait()
+
         @pl.when(t < chunks)
         def _():
-            stage_out(t)
+            out_away(t)
+
+        @pl.when((t < chunks) & (t >= EARLY))
+        def _():
+            out_here(t)
 
         @pl.when((t >= 1) & (t - 1 < chunks))
         def _():
@@ -268,9 +356,11 @@
 
     lax.fori_loop(0, chunks + LAG_MIX, step, 0)
 
-    to_sib.wait_send()
-    for c in first + forwards:
-        c.wait_send()
+    await_bytes(tok.at[pl.ds(0, 2 * far + 1)], tok_send.at[0])
+    if helped:
+        @pl.when(jnp.logical_not(inner))
+        def _():
+            await_bytes(relay, help_send.at[0])
 
     await_bytes(part, rs_send.at[0])
     await_bytes(res.at[:, pl.ds(0, shards - 1)], ag_send.at[0])
@@ -315,9 +405,12 @@
                 pltpu.VMEM((chunks, shards - 1, trows, chunk), bf),
                 pltpu.VMEM((chunks, shards, trows, chunk), bf),
                 pltpu.VMEM((chunks, workers, pr, pc), bf),
+                pltpu.VMEM((HELPED, trows // PIECES, d), bf),
                 dma((3 + chunks,)),
-                dma((2 * far + 1,)),
-                dma((2 * far + 1,)),
+                dma((1,)),
+                dma((1 + 2 * far * PIECES,)),
+                dma((1,)),
+                dma((HELPED,)),
                 dma((1,)),
                 dma((chunks,)),
                 dma((1,)),

time: 368 us -> 360 us (0.978)
  Pallas kernels: 364 us -> 357 us
    pallas_call x1, Pallas kernels: 364 us -> 357 us  [body(): pl.pallas_call(functools.partial(kernel, workers, shards, rs, cs), out_sh...]
where the time goes in v3:
time: 360 us
  Pallas kernels  357 us (99%)
    pallas_call x1, Pallas kernels, body(): pl.pallas_call(functools.partial(kernel, workers, shards, rs, cs), out_sh...  357 us

profile of v3, /device:TPU:0, one launch (start us, length us, event | category | flops | bytes accessed | tf_op | source)
XLA Modules:
  0.0 360.0 jit_solution(3858687874344684178)
XLA Ops:
  0.0 356.9 %shard_map.55 = bf16[1792,2048]{1,0:T(8,128)(2,1)S(1)} custom-call(bf16[256,2048]{1,0:T(8,128)(2,1)} %tokens.1, bf16[256,2048]{1,0:T(8,128)(2,1)} %targets.1, bf16[2048,1792]{1,0:T(8,128)(2,1)} %up_hbm.1, bf16[1792,2048]{1,0:T(8,128)(2,1)} %bitcast.4, s32[3,2,8]{2,1,0:T(2,128)} %bitcast.5), custom_call_target="tpu_custom_call" | custom-call | tf_op jit(solution)/shard_map/pallas_call | solution.py:391
  356.9 3.1 copy.7

commit v4 on v3

--- a/solution.py
+++ b/solution.py
@@ -14,7 +14,7 @@
 LAG_MIX = 4
 PIECES = 8
 HELPED = 3
-EARLY = 3
+EARLY = 2
 ROWTILE = 16
 
 
@@ -152,6 +152,22 @@
         part[j, i - 1] = out_of((me + i) % shards, j).astype(jnp.bfloat16)
         rs_copy(j, i).start()
 
+    mid = trows // 2
+
+    def give_half(i, r0):
+        rows = slice(r0, r0 + mid)
+        v = jnp.dot(hid[(me + i) % shards, rows], w[0], preferred_element_type=jnp.float32) * scale
+        part[0, i - 1, rows] = v.astype(jnp.bfloat16)
+        pltpu.make_async_remote_copy(
+            src_ref=part.at[0, i - 1, pl.ds(r0, mid)], dst_ref=rsl.at[0, i - 1, pl.ds(r0, mid)],
+            send_sem=rs_send.at[0], recv_sem=rs_recv.at[0],
+            device_id={"shard": (me + i) % shards}, device_id_type=MESH).start()
+
+    def far_half(base, d, r0):
+        i = (base - 2 * d + 2 * shards) % shards
+        hidden_of((me + i) % shards, r0, mid)
+        give_half(i, r0)
+
     def out_away(j):
         def one(n, c):
             give_out(j, 1 + n + jnp.where(n + 1 >= near, 1, 0))
@@ -200,18 +216,17 @@
         w_copy(j).wait()
         out_here(j)
         pass_on(range(h * j // EARLY, h * (j + 1) // EARLY))
-    mid = trows // 2
     for d in range(1, far + 1):
-        hidden_of((me - 2 * d + 2 * shards) % shards, 0, mid)
+        far_half(0, d, 0)
     passed_on(range(h))
     for d in range(1, far + 1):
-        hidden_of((sib - 2 * d + 2 * shards) % shards, 0, mid)
+        far_half(near, d, 0)
     pass_on(range(h, PIECES))
     for d in range(1, far + 1):
-        hidden_of((me - 2 * d + 2 * shards) % shards, mid, trows - mid)
+        far_half(0, d, mid)
     passed_on(range(h, PIECES))
     for d in range(1, far + 1):
-        hidden_of((sib - 2 * d + 2 * shards) % shards, mid, trows - mid)
+        far_half(near, d, mid)
 
     tgt_copy.wait()
 
@@ -332,7 +347,7 @@
         def _():
             w_copy(t).wait()
 
-        @pl.when(t < chunks)
+        @pl.when((t >= 1) & (t < chunks))
         def _():
             out_away(t)
 

time: 360 us -> 359 us (level)
  no operation moved by 1% of the time
where the time goes in v4:
time: 359 us
  Pallas kernels  356 us (99%)
    pallas_call x1, Pallas kernels, body(): pl.pallas_call(functools.partial(kernel, workers, shards, rs, cs), out_sh...  356 us

profile of v4, /device:TPU:0, one launch (start us, length us, event | category | flops | bytes accessed | tf_op | source)
XLA Modules:
  0.0 358.6 jit_solution(8344455467486968949)
XLA Ops:
  0.0 355.5 %shard_map.55 = bf16[1792,2048]{1,0:T(8,128)(2,1)S(1)} custom-call(bf16[256,2048]{1,0:T(8,128)(2,1)} %tokens.1, bf16[256,2048]{1,0:T(8,128)(2,1)} %targets.1, bf16[2048,1792]{1,0:T(8,128)(2,1)} %up_hbm.1, bf16[1792,2048]{1,0:T(8,128)(2,1)} %bitcast.4, s32[3,2,8]{2,1,0:T(2,128)} %bitcast.5), custom_call_target="tpu_custom_call" | custom-call | tf_op jit(solution)/shard_map/pallas_call | solution.py:406
  355.5 3.1 copy.7

commit v5 on v4

--- a/solution.py
+++ b/solution.py
@@ -140,7 +140,7 @@
     def rs_copy(j, i):
         return pltpu.make_async_remote_copy(
             src_ref=part.at[j, i - 1], dst_ref=rsl.at[j, i - 1],
-            send_sem=rs_send.at[0], recv_sem=rs_recv.at[j],
+            send_sem=rs_send.at[0], recv_sem=rs_recv.at[jnp.where(j == 0, chunks, j)],
             device_id={"shard": (me + i) % shards}, device_id_type=MESH)
 
     near = (sib - me + shards) % shards
@@ -160,7 +160,7 @@
         part[0, i - 1, rows] = v.astype(jnp.bfloat16)
         pltpu.make_async_remote_copy(
             src_ref=part.at[0, i - 1, pl.ds(r0, mid)], dst_ref=rsl.at[0, i - 1, pl.ds(r0, mid)],
-            send_sem=rs_send.at[0], recv_sem=rs_recv.at[0],
+            send_sem=rs_send.at[0], recv_sem=rs_recv.at[chunks if r0 == 0 else 0],
             device_id={"shard": (me + i) % shards}, device_id_type=MESH).start()
 
     def far_half(base, d, r0):
@@ -245,6 +245,22 @@
         res[j, me] = (total - tgt[:, cols].astype(jnp.float32)).astype(jnp.bfloat16)
         for i in range(1, shards):
             ag_copy(j, i).start()
+
+    def resid_half(r0):
+        if r0 == 0:
+            await_bytes(rsl.at[0, pl.ds(0, shards // 2)], rs_recv.at[chunks])
+        else:
+            await_bytes(rsl.at[0, pl.ds(0, far)], rs_recv.at[0])
+        rows = slice(r0, r0 + mid)
+        total = own[0, rows]
+        for i in range(1, shards):
+            total = total + rsl[0, i - 1, rows].astype(jnp.float32)
+        res[0, me, rows] = (total - tgt[rows, 0:chunk].astype(jnp.float32)).astype(jnp.bfloat16)
+        for i in range(1, shards):
+            pltpu.make_async_remote_copy(
+                src_ref=res.at[0, me, pl.ds(r0, mid)], dst_ref=res.at[0, me, pl.ds(r0, mid)],
+                send_sem=ag_send.at[0], recv_sem=ag_recv.at[0],
+                device_id={"shard": (me + i) % shards}, device_id_type=MESH).start()
 
     def place(k):
         r = pl.ds(pl.multiple_of((k // cs) * pr, 16), pr)
@@ -359,7 +375,7 @@
         def _():
             stage_step(t - 1)
 
-        @pl.when(t < chunks)
+        @pl.when((t >= 1) & (t < chunks))
         def _():
             stage_resid(t)
 
@@ -369,6 +385,8 @@
 
         return c
 
+    resid_half(0)
+    resid_half(mid)
     lax.fori_loop(0, chunks + LAG_MIX, step, 0)
 
     await_bytes(tok.at[pl.ds(0, 2 * far + 1)], tok_send.at[0])
@@ -427,7 +445,7 @@
                 dma((1,)),
                 dma((HELPED,)),
                 dma((1,)),
-                dma((chunks,)),
+                dma((chunks + 1,)),
                 dma((1,)),
                 dma((chunks,)),
                 dma((1,)),

time: 359 us -> 359 us (level)
  no operation moved by 1% of the time
where the time goes in v5:
time: 359 us
  Pallas kernels  356 us (99%)
    pallas_call x1, Pallas kernels, body(): pl.pallas_call(functools.partial(kernel, workers, shards, rs, cs), out_sh...  356 us

profile of v5, /device:TPU:0, one launch (start us, length us, event | category | flops | bytes accessed | tf_op | source)
XLA Modules:
  0.0 358.9 jit_solution(10950728134307961995)
XLA Ops:
  0.0 355.9 %shard_map.55 = bf16[1792,2048]{1,0:T(8,128)(2,1)S(1)} custom-call(bf16[256,2048]{1,0:T(8,128)(2,1)} %tokens.1, bf16[256,2048]{1,0:T(8,128)(2,1)} %targets.1, bf16[2048,1792]{1,0:T(8,128)(2,1)} %up_hbm.1, bf16[1792,2048]{1,0:T(8,128)(2,1)} %bitcast.4, s32[3,2,8]{2,1,0:T(2,128)} %bitcast.5), custom_call_target="tpu_custom_call" | custom-call | tf_op jit(solution)/shard_map/pallas_call | solution.py:424
  355.9 3.1 copy.7
